TPU v7x, 128 devices: a whole 4x4x4 slice. The times are simulated.
128 devices in a mesh: seq: 128 (over y, x, z, core).
Axes of the slice: x: 4, y: 4, z: 4, core: 2. Of those that a mesh axis runs over, the one named last changes fastest.
Arguments:
- inputs: bfloat16 [16384, 4096], P('seq'), may hold values from -6 to 6
- step_sizes: bfloat16 [16384, 4096], P('seq'), may hold values from 0.25 to 2
- cotangent: bfloat16 [16384, 4096], P('seq'), may hold values from -6 to 6
- input_coeffs: float32 [16, 16384], P(None, 'seq'), may hold values from -0.3 to 0.3
- output_coeffs: float32 [16, 16384], P(None, 'seq'), may hold values from -0.3 to 0.3
- decay_rates: float32 [16, 4096], replicated, as said below
Outputs:
- grad_inputs: bfloat16 [16384, 4096], P('seq')
- grad_steps: bfloat16 [16384, 4096], P('seq')
- grad_in_coeffs: float32 [16, 16384], P(None, 'seq')
- grad_out_coeffs: float32 [16, 16384], P(None, 'seq')
- grad_rates: float32 [16, 4096], P(None, 'seq')
Inputs may be any that keep to these rules, and one draw needn't show every extreme that they name: `decay_rates`: every entry lies between 0.1 / 16384 and 0.15.
All inputs are finite; a program needn't handle non-finite values.
Results may differ from a plain program's by a relative error of at most 0.001.
Values sent between devices are 32-bit elements; how exact they have to be, the bound alone decides.
A program may use at most 64 MiB of HBM per device.

v0:
```python
from functools import partial
import math

import jax
import jax.numpy as jnp
from jax import lax
from jax.experimental import pallas as pl
from jax.experimental.pallas import tpu as pltpu
from jax.sharding import PartitionSpec as P

LANES = 128
SUB = 8
TILES = 4
GROUP = 8
LOG2E = math.log2(math.e)
LN2 = math.log(2.0)
F32 = jnp.float32
MESH = pl.DeviceIdType.MESH


def expand(coef_ref, wide, tokens, n_state):
    for t in range(tokens):
        wide[t] = jnp.broadcast_to(coef_ref[:, t : t + 1], (n_state, LANES))


def row(ref, t, n_state):
    return ref[:, pl.ds(t, n_state, stride=0), :]


def lanes_of(k):
    return slice(k * LANES, (k + 1) * LANES)


def loop(start, stop, body):
    def step(k, _):
        body(k)
        return 0

    lax.fori_loop(start, stop, step, 0)


def lane_sums(acc, out_ref, tokens, n_state):
    lane = lax.broadcasted_iota(jnp.int32, (n_state, tokens), 1)
    total = jnp.zeros((n_state, tokens), F32)
    for t in range(tokens):
        total = jnp.where(lane == t, jnp.sum(acc[t], axis=1, keepdims=True), total)
    out_ref[...] = total


def whole_kernel(
    n, block,
    x_ref, d_ref, g_ref, b_ref, c_ref, a_ref,
    gi_ref, gs_ref, gb_ref, gc_ref, gr_ref,
    bx, cx, dl, xx, uu, gg, rt, st, hs, dec, accb, accc, csp, awp, gi, gs,
    out1, in1, out2, in2, out3, in3, send1, recv1, send2, recv2, send3, recv3,
):
    me = lax.axis_index("seq")
    tokens, channels = x_ref.shape
    n_state = a_ref.shape[0]
    tiles, width = block // LANES, channels // n
    blocks, owners = channels // block, block // width
    home = me // owners
    barrier = pltpu.get_barrier_semaphore()

    def tell(k):
        pl.semaphore_signal(barrier, inc=1, device_id=(lax.rem(me + k, n),), device_id_type=MESH)

    def copy(src, dst, send_sem, recv_sem, dest, slot):
        return pltpu.make_async_remote_copy(
            src_ref=src.at[dest],
            dst_ref=dst.at[slot],
            send_sem=send_sem.at[dest],
            recv_sem=recv_sem.at[slot],
            device_id=(dest,),
            device_id_type=MESH,
        )

    first = (out1, in1, send1, recv1)
    second = (out2, in2, send2, recv2)
    third = (out3, in3, send3, recv3)

    def stage(b):
        for k in range(tiles):
            lanes = pl.ds(pl.multiple_of(b * block + k * LANES, LANES), LANES)
            delta = d_ref[:, lanes].astype(F32)
            x = x_ref[:, lanes].astype(F32)
            dl[k] = delta
            xx[k] = x
            uu[k] = delta * x
            gg[k] = g_ref[:, lanes].astype(F32)
            rt[k] = a_ref[:, lanes] * (-LOG2E)

    loop(1, n, tell)
    expand(b_ref, bx, tokens, n_state)
    expand(c_ref, cx, tokens, n_state)
    accb[...] = jnp.zeros_like(accb)
    accc[...] = jnp.zeros_like(accc)
    state_shape = (tiles, n_state, LANES)

    def summarize(order):
        b = lax.rem(home + 1 + order, blocks)
        stage(b)
        rates = rt[...]

        def group(i, carry):
            prod, end, back = carry
            for s in range(GROUP):
                t = i * GROUP + s
                decay = jnp.exp2(row(dl, t, n_state) * rates)
                end = decay * end + bx[t][None] * row(uu, t, n_state)
                prod = decay * prod
                back = back + prod * (cx[t][None] * row(gg, t, n_state))
            return prod, end, back

        zero = jnp.zeros(state_shape, F32)
        _, end, back = lax.fori_loop(
            0, tokens // GROUP, group, (jnp.ones(state_shape, F32), zero, zero)
        )
        for k in range(tiles):
            st[:n_state, lanes_of(k)] = end[k]
            st[n_state : 2 * n_state, lanes_of(k)] = back[k]
            st[2 * n_state :, lanes_of(k)] = jnp.broadcast_to(
                jnp.sum(dl[k], axis=0, keepdims=True), (1, LANES)
            )

        @pl.when(order == 0)
        def _():
            pl.semaphore_wait(barrier, n - 1)

        for j in range(owners):
            dest = b * owners + j
            out1[dest] = st[:, j * width : (j + 1) * width]

            @pl.when(dest != me)
            def _():
                copy(*first, dest, me).start()

    loop(0, blocks, summarize)
    in1[me] = out1[me]

    def arrived(refs):
        def wait(k):
            origin = lax.rem(me + n - k, n)
            copy(*refs, origin, origin).wait_recv()

        loop(1, n, wait)

    arrived(first)
    if width % LANES == 0:
        own = a_ref[:, pl.ds(pl.multiple_of(me * width, LANES), width)] * (-LOG2E)
    else:
        own = jnp.zeros((n_state, width), F32)
        for j in range(n):
            own = jnp.where(me == j, a_ref[:, j * width : (j + 1) * width] * (-LOG2E), own)

    def scan(i, carry):
        ahead, behind = carry
        d, e = i, n - 1 - i
        out2[d, :n_state, :] = ahead
        out2[e, n_state:, :] = behind
        ahead = jnp.exp2(own * in1[d, 2 * n_state : 2 * n_state + 1, :]) * ahead + in1[d, :n_state, :]
        behind = (
            jnp.exp2(own * in1[e, 2 * n_state : 2 * n_state + 1, :]) * behind
            + in1[e, n_state : 2 * n_state, :]
        )
        return ahead, behind

    blank = jnp.zeros((n_state, width), F32)
    lax.fori_loop(0, n, scan, (blank, blank), unroll=4)
    loop(1, n, lambda k: copy(*second, lax.rem(me + n - k, n), me).start())
    in2[me] = out2[me]

    def differentiate(order, _):
        b = lax.rem(home + order, blocks)
        stage(b)
        for j in range(owners):
            origin = b * owners + j

            @pl.when(origin != me)
            def _():
                copy(*second, origin, origin).wait_recv()

            st[: 2 * n_state, j * width : (j + 1) * width] = in2[origin]
        rates = rt[...]

        def ahead(i, hidden):
            for s in range(GROUP):
                t = i * GROUP + s
                decay = jnp.exp2(row(dl, t, n_state) * rates)
                dec[t] = decay
                hs[t] = hidden
                hidden = decay * hidden + bx[t][None] * row(uu, t, n_state)
                accc[t] += jnp.sum(row(gg, t, n_state) * hidden, axis=0)
            return hidden

        start = jnp.stack([st[:n_state, lanes_of(k)] for k in range(tiles)])
        lax.fori_loop(0, tokens // GROUP, ahead, start)

        def behind(i, carry):
            later, rate = carry
            base = tokens - GROUP - i * GROUP
            for s in reversed(range(GROUP)):
                t = base + s
                bs = bx[t][None]
                state = cx[t][None] * row(gg, t, n_state) + later
                later = dec[t] * state
                weighted = later * hs[t]
                rate = rate + weighted * row(dl, t, n_state)
                one, two = state * bs, weighted * rates
                fold = slice(s * SUB, (s + 1) * SUB)
                csp[:, fold, :] = sum(one[:, h : h + SUB] for h in range(0, n_state, SUB))
                awp[:, fold, :] = sum(two[:, h : h + SUB] for h in range(0, n_state, SUB))
                accb[t] += jnp.sum(state * row(uu, t, n_state), axis=0)
            rows = pl.ds(pl.multiple_of(base, GROUP), GROUP)
            coeff = csp[:, pl.ds(0, GROUP, stride=SUB), :]
            weigh = awp[:, pl.ds(0, GROUP, stride=SUB), :]
            for s in range(1, SUB):
                coeff = coeff + csp[:, pl.ds(s, GROUP, stride=SUB), :]
                weigh = weigh + awp[:, pl.ds(s, GROUP, stride=SUB), :]
            gi[:, rows, :] = dl[:, rows, :] * coeff
            gs[:, rows, :] = xx[:, rows, :] * coeff + LN2 * weigh
            return later, rate

        last = jnp.stack([st[n_state : 2 * n_state, lanes_of(k)] for k in range(tiles)])
        _, rate = lax.fori_loop(
            0, tokens // GROUP, behind, (last, jnp.zeros(state_shape, F32))
        )
        for k in range(tiles):
            lanes = pl.ds(pl.multiple_of(b * block + k * LANES, LANES), LANES)
            gi_ref[:, lanes] = gi[k].astype(gi_ref.dtype)
            gs_ref[:, lanes] = gs[k].astype(gs_ref.dtype)
            st[:n_state, lanes_of(k)] = -rate[k]
        for j in range(owners):
            dest = b * owners + j
            out3[dest] = st[:n_state, j * width : (j + 1) * width]

            @pl.when(dest != me)
            def _():
                copy(*third, dest, me).start()

        return 0

    lax.fori_loop(0, blocks, differentiate, 0)
    in3[me] = out3[me]
    lane_sums(accb, gb_ref, tokens, n_state)
    lane_sums(accc, gc_ref, tokens, n_state)
    arrived(third)
    gr_ref[...] = lax.fori_loop(0, n, lambda d, total: total + in3[d], blank)
    for refs in (first, second, third):
        loop(1, n, lambda k: copy(*refs, lax.rem(me + k, n), me).wait_send())


def shards(n, inputs, step_sizes, cotangent, input_coeffs, output_coeffs, decay_rates):
    n_state, channels = decay_rates.shape
    tokens = inputs.shape[0]
    width = channels // n
    block = max(TILES * LANES, width)
    tiles = block // LANES
    wide = pltpu.VMEM((tokens, n_state, LANES), F32)
    rows = pltpu.VMEM((tiles, tokens, LANES), F32)
    states = pltpu.VMEM((tokens, tiles, n_state, LANES), F32)
    fold = pltpu.VMEM((tiles, GROUP * SUB, LANES), F32)
    vmem = pl.BlockSpec(memory_space=pltpu.VMEM)
    dma = pltpu.SemaphoreType.DMA((n,))
    head_rows = 2 * n_state + 1
    slots = lambda count: [pltpu.VMEM((n, count, width), F32)] * 2
    return pl.pallas_call(
        partial(whole_kernel, n, block),
        name="whole",
        in_specs=[vmem] * 6,
        out_specs=[vmem] * 5,
        out_shape=[
            jax.ShapeDtypeStruct((tokens, channels), jnp.bfloat16),
            jax.ShapeDtypeStruct((tokens, channels), jnp.bfloat16),
            jax.ShapeDtypeStruct((n_state, tokens), F32),
            jax.ShapeDtypeStruct((n_state, tokens), F32),
            jax.ShapeDtypeStruct((n_state, width), F32),
        ],
        scratch_shapes=[
            wide, wide, rows, rows, rows, rows,
            pltpu.VMEM((tiles, n_state, LANES), F32),
            pltpu.VMEM((head_rows, block), F32),
            states, states, wide, wide, fold, fold, rows, rows,
            *slots(head_rows), *slots(2 * n_state), *slots(n_state),
            dma, dma, dma, dma, dma, dma,
        ],
        compiler_params=pltpu.CompilerParams(
            collective_id=0, has_side_effects=True, vmem_limit_bytes=60 * 1024 * 1024
        ),
    )(inputs, step_sizes, cotangent, input_coeffs, output_coeffs, decay_rates)


def solution(mesh):
    placed = (P("seq", None), P("seq", None), P("seq", None), P(None, "seq"), P(None, "seq"), P())
    return jax.shard_map(
        partial(shards, mesh.shape["seq"]),
        mesh=mesh,
        in_specs=placed,
        out_specs=(P("seq", None), P("seq", None), P(None, "seq"), P(None, "seq"), P(None, "seq")),
        check_vma=False,
    )
```

profile of v0, /device:TPU:1, one launch (start us, length us, event | category | flops | bytes accessed | tf_op | source)
XLA Modules:
  0.0 159.6 jit_solution(9463576457528525312)
XLA Ops:
  0.6 153.6 %whole.1 = (bf16[128,4096]{1,0:T(8,128)(2,1)}, bf16[128,4096]{1,0:T(8,128)(2,1)}, f32[16,128]{1,0:T(8,128)}, f32[16,128]{1,0:T(8,128)}, f32[16,32]{1,0:T(8,128)}) custom-call(bf16[128,4096]{1,0:T(8,128)(2,1)} %x_ref.1, bf16[128,4096]{1,0:T(8,128)(2,1)} %d_ref.1, bf16[128,4096]{1,0:T(8,128)(2,1)} %g_ref.1, f32[16,128]{1,0:T(8,128)} %b_ref.1, ...), custom_call_target="tpu_custom_call" | custom-call | tf_op jit(solution)/shard_map/whole/pallas_call | solution.py:267
  154.3 0.0 copy-start
  154.3 2.4 %copy.16 = bf16[128,4096]{1,0:T(8,128)(2,1)} copy(bf16[128,4096]{1,0:T(8,128)(2,1)} %get-tuple-element.10) | data formatting | bytes 2097152
  156.7 0.0 copy-done
  156.7 0.0 copy-start.3
  156.7 1.0 copy.17
  157.6 0.0 copy-done.3
  157.6 0.0 copy-start.2
  157.6 0.6 copy.18
  158.2 0.1 copy-done.2
  158.3 0.0 copy-start.1
  158.3 0.6 copy.19
  158.9 0.1 copy-done.1
  159.0 0.6 copy.20
Async XLA Ops:
  154.3 2.4 %copy-start = (bf16[128,4096]{1,0:T(8,128)(2,1)S(1)}, bf16[128,4096]{1,0:T(8,128)(2,1)}, u32[]{:S(2)}) copy-start(bf16[128,4096]{1,0:T(8,128)(2,1)} %get-tuple-element.11) | copy-start | bytes 3145732
  156.7 1.0 copy-start.3
  157.6 0.7 copy-start.2
  158.3 0.7 copy-start.1
where the time goes:
time: 163 us; the launch traced here: 160 us
  Pallas kernels  154 us (94%)
  local copies, waits for them, and re-layouts  5.35 us (3%)
    pallas_call x1, Pallas kernels, shards(): pl.pallas_call(partial(whole_kernel, n, block), name='whole', in_specs=[v...  154 us
    unnamed x13, local copies, waits for them, and re-layouts  5.35 us

commit v1 on v0

v1 whole, which is shorter than its diff:
```python
from functools import partial
import math

import jax
import jax.numpy as jnp
from jax import lax
from jax.experimental import pallas as pl
from jax.experimental.pallas import tpu as pltpu
from jax.sharding import PartitionSpec as P

LANES = 128
SUB = 8
TILES = 4
GROUP = 8
PAIR = 16
CHUNKS = 2
LOG2E = math.log2(math.e)
LN2 = math.log(2.0)
F32 = jnp.float32
MESH = pl.DeviceIdType.MESH


def expand(coef_ref, wide, tokens, n_state):
    for t in range(tokens):
        wide[t] = jnp.broadcast_to(coef_ref[:, t : t + 1], (n_state, LANES))


def loop(start, stop, body):
    def step(k, _):
        body(k)
        return 0

    lax.fori_loop(start, stop, step, 0)


def lane_sums(acc, out_ref, tokens, n_state):
    lane = lax.broadcasted_iota(jnp.int32, (n_state, tokens), 1)
    total = jnp.zeros((n_state, tokens), F32)
    for t in range(tokens):
        total = jnp.where(lane == t, jnp.sum(acc[t], axis=1, keepdims=True), total)
    out_ref[...] = total


def whole_kernel(
    n,
    x_ref, d_ref, g_ref, b_ref, c_ref, a_ref,
    gi_ref, gs_ref, gb_ref, gc_ref, gr_ref,
    bx, cx, dl, uu, gg, dec, hs, accb, accc, csp, awp, st, rt, pk,
    out1, in1, out2, in2, out3, in3, send1, recv1, send2, recv2, send3, recv3,
):
    me = lax.axis_index("seq")
    tokens, channels = x_ref.shape
    n_state = a_ref.shape[0]
    all_tiles = channels // LANES
    chunk_tiles = all_tiles // CHUNKS
    chunk_blocks = chunk_tiles // TILES
    owners = n // chunk_tiles
    rows = n_state // owners
    parts = n // all_tiles
    width = LANES // parts
    home = me // (TILES * owners)
    barrier = pltpu.get_barrier_semaphore()

    def tell(k):
        pl.semaphore_signal(barrier, inc=1, device_id=(lax.rem(me + k, n),), device_id_type=MESH)

    def copy(src, dst, send_sem, recv_sem, dest):
        return pltpu.make_async_remote_copy(
            src_ref=src, dst_ref=dst, send_sem=send_sem, recv_sem=recv_sem,
            device_id=(dest,), device_id_type=MESH,
        )

    def settle(ref, sem):
        pltpu.make_async_copy(ref, ref, sem).wait()

    def row(ref, first, t):
        return ref[pl.ds(first, TILES), pl.ds(t, n_state, stride=0), :]

    def lanes_at(tile):
        return pl.ds(pl.multiple_of(tile * LANES, LANES), LANES)

    def rates_of(first):
        for k in range(TILES):
            rt[k] = a_ref[:, lanes_at(first + k)] * (-LOG2E)
        return rt[...]

    loop(1, n, tell)
    expand(b_ref, bx, tokens, n_state)
    expand(c_ref, cx, tokens, n_state)
    accb[...] = jnp.zeros_like(accb)
    accc[...] = jnp.zeros_like(accc)
    state_shape = (TILES, n_state, LANES)
    zero = jnp.zeros(state_shape, F32)

    def first_out(c, dest):
        return out1.at[c, dest, pl.ds(0, 2 * rows + 1)]

    def summarize(c, order):
        b = c * chunk_blocks + lax.rem(home + 1 + order, chunk_blocks)
        first = b * TILES
        for k in range(TILES):
            lanes = lanes_at(first + k)
            delta = d_ref[:, lanes].astype(F32)
            dl[first + k] = delta
            uu[first + k] = delta * x_ref[:, lanes].astype(F32)
            gg[first + k] = g_ref[:, lanes].astype(F32)
        rates = rates_of(first)

        def forth(i, end):
            for s in range(GROUP):
                t = i * GROUP + s
                decay = jnp.exp2(row(dl, first, t) * rates)
                dec[b, t] = decay
                end = decay * end + bx[t][None] * row(uu, first, t)
            return end

        st[0] = lax.fori_loop(0, tokens // GROUP, forth, zero)

        def back(i, later):
            for s in range(GROUP):
                t = tokens - 1 - i * GROUP - s
                later = dec[b, t] * (cx[t][None] * row(gg, first, t) + later)
            return later

        st[1] = lax.fori_loop(0, tokens // GROUP, back, zero)
        for k in range(TILES):
            spent = jnp.sum(dl[first + k], axis=0, keepdims=True)
            for j in range(owners):
                dest = (lax.rem(home + 1 + order, chunk_blocks) * TILES + k) * owners + j
                out1[c, dest, :rows] = st[0, k, j * rows : (j + 1) * rows]
                out1[c, dest, rows : 2 * rows] = st[1, k, j * rows : (j + 1) * rows]
                out1[c, dest, 2 * rows : 2 * rows + 1] = spent

        if c == 0:
            @pl.when(order == 0)
            def _():
                pl.semaphore_wait(barrier, n - 1)

        def send(j):
            dest = lax.rem(home + 1 + order, chunk_blocks) * TILES * owners + j

            @pl.when(dest != me)
            def _():
                copy(
                    first_out(c, dest), in1.at[c, me, pl.ds(0, 2 * rows + 1)],
                    send1.at[c], recv1.at[c], dest,
                ).start()

        loop(0, TILES * owners, send)

    def propagate(c):
        in1[c, me] = out1[c, me]
        settle(in1.at[c, pl.ds(0, n - 1), pl.ds(0, 2 * rows + 1)], recv1.at[c])
        mine = a_ref[:, lanes_at(c * chunk_tiles + me // owners)] * (-LOG2E)
        own = jnp.zeros((rows, LANES), F32)
        for j in range(owners):
            own = jnp.where(lax.rem(me, owners) == j, mine[j * rows : (j + 1) * rows], own)
        own = jnp.concatenate([own, own], axis=0)
        upper = lax.broadcasted_iota(jnp.int32, (2 * rows, LANES), 0) < rows

        def scan(i, state):
            e = n - 1 - i
            out2[c, i, :rows] = state[:rows]
            out2[c, e, rows : 2 * rows] = state[rows:]
            spent = jnp.where(
                upper,
                in1[c, i, pl.ds(2 * rows, 2 * rows, stride=0), :],
                in1[c, e, pl.ds(2 * rows, 2 * rows, stride=0), :],
            )
            term = jnp.where(upper, in1[c, i, : 2 * rows], in1[c, e, : 2 * rows])
            return jnp.exp2(own * spent) * state + term

        lax.fori_loop(0, n, scan, jnp.zeros((2 * rows, LANES), F32), unroll=8)

        def send(k):
            dest = lax.rem(me + n - k, n)
            copy(
                out2.at[c, dest, pl.ds(0, 2 * rows)], in2.at[c, me, pl.ds(0, 2 * rows)],
                send2.at[c], recv2.at[c], dest,
            ).start()

        loop(1, n, send)
        in2[c, me] = out2[c, me]

    lane_group = lax.broadcasted_iota(jnp.int32, (SUB, LANES), 1) // width
    low_lanes = lax.broadcasted_iota(jnp.int32, (SUB // 2, LANES), 1) < LANES // 2

    def differentiate(c, order):
        local = lax.rem(home + order, chunk_blocks)
        b = c * chunk_blocks + local
        first = b * TILES
        for k in range(TILES):
            for j in range(owners):
                origin = (local * TILES + k) * owners + j
                st[0, k, j * rows : (j + 1) * rows] = in2[c, origin, :rows]
                st[1, k, j * rows : (j + 1) * rows] = in2[c, origin, rows : 2 * rows]
        rates = rates_of(first)

        def ahead(i, hidden):
            for s in range(GROUP):
                t = i * GROUP + s
                hs[t] = hidden
                hidden = dec[b, t] * hidden + bx[t][None] * row(uu, first, t)
                accc[t] += jnp.sum(row(gg, first, t) * hidden, axis=0)
            return hidden

        lax.fori_loop(0, tokens // GROUP, ahead, st[0])

        def behind(i, carry):
            later, rate = carry
            base = tokens - PAIR - i * PAIR
            for s in reversed(range(PAIR)):
                t = base + s
                state = cx[t][None] * row(gg, first, t) + later
                later = dec[b, t] * state
                weighted = later * hs[t]
                rate = rate + weighted * row(dl, first, t)
                one, two = state * bx[t][None], weighted * rates
                fold = slice(s * SUB, (s + 1) * SUB)
                csp[:, fold, :] = one[:, :SUB] + one[:, SUB:]
                awp[:, fold, :] = two[:, :SUB] + two[:, SUB:]
                accb[t] += jnp.sum(state * row(uu, first, t), axis=0)
            tok = pl.ds(pl.multiple_of(base, PAIR), PAIR)
            for k in range(TILES):
                coeff = csp[k, pl.ds(0, PAIR, stride=SUB), :]
                weigh = awp[k, pl.ds(0, PAIR, stride=SUB), :]
                for s in range(1, SUB):
                    coeff = coeff + csp[k, pl.ds(s, PAIR, stride=SUB), :]
                    weigh = weigh + awp[k, pl.ds(s, PAIR, stride=SUB), :]
                lanes = lanes_at(first + k)
                x = x_ref[tok, lanes].astype(F32)
                gi_ref[tok, lanes] = (dl[first + k, tok, :] * coeff).astype(gi_ref.dtype)
                gs_ref[tok, lanes] = (x * coeff + LN2 * weigh).astype(gs_ref.dtype)
            return later, rate

        _, rate = lax.fori_loop(0, tokens // PAIR, behind, (st[1], zero))
        for k in range(TILES):
            halves = (-rate[k, :SUB], -rate[k, SUB:])
            turned = [
                [v if s == 0 else pltpu.roll(v, s * width, axis=1) for s in range(parts)]
                for v in halves
            ]
            for j in range(parts):
                packed = turned[0][(0 - j) % parts]
                for g in range(1, parts):
                    packed = jnp.where(lane_group == g, turned[g % 2][(g - j) % parts], packed)
                pk[k * parts + j] = packed
        for k in range(TILES):
            for j in range(parts):
                dest = (first + k) * parts + j
                slot = k * parts + j
                out3[dest] = jnp.where(low_lanes, pk[slot, : SUB // 2], pk[slot, SUB // 2 :])

        def send(j):
            dest = first * parts + j

            @pl.when(dest != me)
            def _():
                copy(out3.at[dest], in3.at[me], send3.at[0], recv3.at[0], dest).start()

        loop(0, TILES * parts, send)

    for c in range(CHUNKS):
        loop(0, chunk_blocks, partial(summarize, c))
    for c in range(CHUNKS):
        propagate(c)
    for c in range(CHUNKS):
        settle(in2.at[c, pl.ds(0, n - 1), pl.ds(0, 2 * rows)], recv2.at[c])
        loop(0, chunk_blocks, partial(differentiate, c))
    in3[me] = out3[me]
    lane_sums(accb, gb_ref, tokens, n_state)
    lane_sums(accc, gc_ref, tokens, n_state)
    settle(in3.at[pl.ds(0, n - 1)], recv3.at[0])
    blank = jnp.zeros((SUB // 2, LANES), F32)
    total = lax.fori_loop(0, n, lambda d, total: total + in3[d], blank, unroll=8)
    gr_ref[0:4, :] = total[:, :width]
    gr_ref[4:8, :] = total[:, 2 * width : 3 * width]
    gr_ref[8:12, :] = total[:, width : 2 * width]
    gr_ref[12:16, :] = total[:, 3 * width :]
    for c in range(CHUNKS):
        settle(out1.at[c, pl.ds(0, n - 1), pl.ds(0, 2 * rows + 1)], send1.at[c])
        settle(out2.at[c, pl.ds(0, n - 1), pl.ds(0, 2 * rows)], send2.at[c])
    settle(out3.at[pl.ds(0, n - 1)], send3.at[0])


def shards(n, inputs, step_sizes, cotangent, input_coeffs, output_coeffs, decay_rates):
    n_state, channels = decay_rates.shape
    tokens = inputs.shape[0]
    all_tiles = channels // LANES
    blocks = all_tiles // TILES
    parts = n // all_tiles
    wide = pltpu.VMEM((tokens, n_state, LANES), F32)
    flat = pltpu.VMEM((all_tiles, tokens, LANES), F32)
    fold = pltpu.VMEM((TILES, PAIR * SUB, LANES), F32)
    vmem = pl.BlockSpec(memory_space=pltpu.VMEM)
    slots = pltpu.VMEM((CHUNKS, n, SUB, LANES), F32)
    small = pltpu.VMEM((n, SUB // 2, LANES), F32)
    each = pltpu.SemaphoreType.DMA((CHUNKS,))
    one = pltpu.SemaphoreType.DMA((1,))
    return pl.pallas_call(
        partial(whole_kernel, n),
        name="whole",
        in_specs=[vmem] * 6,
        out_specs=[vmem] * 5,
        out_shape=[
            jax.ShapeDtypeStruct((tokens, channels), jnp.bfloat16),
            jax.ShapeDtypeStruct((tokens, channels), jnp.bfloat16),
            jax.ShapeDtypeStruct((n_state, tokens), F32),
            jax.ShapeDtypeStruct((n_state, tokens), F32),
            jax.ShapeDtypeStruct((n_state, channels // n), F32),
        ],
        scratch_shapes=[
            wide, wide, flat, flat, flat,
            pltpu.VMEM((blocks, tokens, TILES, n_state, LANES), F32),
            pltpu.VMEM((tokens, TILES, n_state, LANES), F32),
            wide, wide, fold, fold,
            pltpu.VMEM((2, TILES, n_state, LANES), F32),
            pltpu.VMEM((TILES, n_state, LANES), F32),
            pltpu.VMEM((TILES * parts, SUB, LANES), F32),
            slots, slots, slots, slots, small, small,
            each, each, each, each, one, one,
        ],
        compiler_params=pltpu.CompilerParams(
            collective_id=0, has_side_effects=True, vmem_limit_bytes=63 * 1024 * 1024
        ),
    )(inputs, step_sizes, cotangent, input_coeffs, output_coeffs, decay_rates)


def solution(mesh):
    placed = (P("seq", None), P("seq", None), P("seq", None), P(None, "seq"), P(None, "seq"), P())
    return jax.shard_map(
        partial(shards, mesh.shape["seq"]),
        mesh=mesh,
        in_specs=placed,
        out_specs=(P("seq", None), P("seq", None), P(None, "seq"), P(None, "seq"), P(None, "seq")),
        check_vma=False,
    )
```

time: 163 us -> 76 us (0.47)
  the two profiles are of different devices: /device:TPU:1 before, /device:TPU:31 now
where the time goes in v1:
time: 76 us; the launch traced here: 75.8 us
  Pallas kernels  69.8 us (92%)
  local copies, waits for them, and re-layouts  5.35 us (7%)
    pallas_call x1, Pallas kernels, shards(): pl.pallas_call(partial(whole_kernel, n), name='whole', in_specs=[vmem] *...  69.8 us
    unnamed x13, local copies, waits for them, and re-layouts  5.35 us

profile of v1, /device:TPU:31, one launch (start us, length us, event | category | flops | bytes accessed | tf_op | source)
XLA Modules:
  0.0 75.8 jit_solution(11484433187886400927)
XLA Ops:
  0.6 69.8 %whole.1 = (bf16[128,4096]{1,0:T(8,128)(2,1)}, bf16[128,4096]{1,0:T(8,128)(2,1)}, f32[16,128]{1,0:T(8,128)}, f32[16,128]{1,0:T(8,128)}, f32[16,32]{1,0:T(8,128)}) custom-call(bf16[128,4096]{1,0:T(8,128)(2,1)} %x_ref.1, bf16[128,4096]{1,0:T(8,128)(2,1)} %d_ref.1, bf16[128,4096]{1,0:T(8,128)(2,1)} %g_ref.1, f32[16,128]{1,0:T(8,128)} %b_ref.1, ...), custom_call_target="tpu_custom_call" | custom-call | tf_op jit(solution)/shard_map/whole/pallas_call | solution.py:300
  70.4 0.0 copy-start
  70.5 2.4 %copy.16 = bf16[128,4096]{1,0:T(8,128)(2,1)} copy(bf16[128,4096]{1,0:T(8,128)(2,1)} %get-tuple-element.10) | data formatting | bytes 2097152
  72.8 0.0 copy-done
  72.8 0.0 copy-start.3
  72.8 1.0 %copy.17 = bf16[128,4096]{1,0:T(8,128)(2,1)} copy(bf16[128,4096]{1,0:T(8,128)(2,1)S(1)} %copy-done) | data formatting | bytes 2097152
  73.8 0.0 copy-done.3
  73.8 0.0 copy-start.2
  73.8 0.6 copy.18
  74.4 0.1 copy-done.2
  74.5 0.0 copy-start.1
  74.5 0.6 copy.19
  75.1 0.1 copy-done.1
  75.2 0.6 copy.20
Async XLA Ops:
  70.4 2.4 %copy-start = (bf16[128,4096]{1,0:T(8,128)(2,1)S(1)}, bf16[128,4096]{1,0:T(8,128)(2,1)}, u32[]{:S(2)}) copy-start(bf16[128,4096]{1,0:T(8,128)(2,1)} %get-tuple-element.11) | copy-start | bytes 3145732
  72.8 1.0 %copy-start.3 = (f32[16,128]{1,0:T(8,128)S(1)}, f32[16,128]{1,0:T(8,128)}, u32[]{:S(2)}) copy-start(f32[16,128]{1,0:T(8,128)} %get-tuple-element.12) | copy-start | bytes 24580
  73.8 0.7 copy-start.2
  74.5 0.7 copy-start.1

commit v2 on v1

v2 whole, which is shorter than its diff:
```python
from functools import partial
import math

import jax
import jax.numpy as jnp
from jax import lax
from jax.experimental import pallas as pl
from jax.experimental.pallas import tpu as pltpu
from jax.sharding import PartitionSpec as P

LANES = 128
SUB = 8
TILES = 4
GROUP = 8
FORTH = 16
BACK = 16
AHEAD = 16
PAIR = 32
CHUNKS = 4
LOG2E = math.log2(math.e)
LN2 = math.log(2.0)
F32 = jnp.float32
MESH = pl.DeviceIdType.MESH


def loop(start, stop, body):
    def step(k, _):
        body(k)
        return 0

    lax.fori_loop(start, stop, step, 0)


def lane_sums(acc, out_ref, tokens, n_state):
    lane = lax.broadcasted_iota(jnp.int32, (n_state, tokens), 1)
    total = jnp.zeros((n_state, tokens), F32)
    for t in range(tokens):
        total = jnp.where(lane == t, jnp.sum(acc[t], axis=1, keepdims=True), total)
    out_ref[...] = total


def whole_kernel(
    n,
    x_hbm, d_hbm, g_hbm, b_hbm, c_hbm, a_hbm,
    giv, gsv, gb_ref, gc_ref, gr_ref,
    xv, dv, gv, bv, cv, av,
    bx, cx, dl, uu, gg, dec, hs, accb, accc, csp, awp, rt, pk,
    out1, in1, out2, in2, out3, in3,
    send1, recv1, send2, recv2, send3, recv3, load, small_load,
):
    me = lax.axis_index("seq")
    tokens, channels = xv.shape
    n_state = av.shape[0]
    all_tiles = channels // LANES
    blocks = all_tiles // TILES
    chunk_tiles = all_tiles // CHUNKS
    chunk_blocks = chunk_tiles // TILES
    parts = n // all_tiles
    width = LANES // parts
    partner = me + 1 - 2 * lax.rem(me, 2)
    barrier = pltpu.get_barrier_semaphore()

    def copy(src, dst, send_sem, recv_sem, dest):
        return pltpu.make_async_remote_copy(
            src_ref=src, dst_ref=dst, send_sem=send_sem, recv_sem=recv_sem,
            device_id=(dest,), device_id_type=MESH,
        )

    def settle(ref, sem):
        pltpu.make_async_copy(ref, ref, sem).wait()

    def row(ref, first, t):
        return ref[pl.ds(first, TILES), pl.ds(t, n_state, stride=0), :]

    def lanes_at(tile, count=1):
        return pl.ds(pl.multiple_of(tile * LANES, LANES), count * LANES)

    def slot(index, count):
        return pl.ds(pl.multiple_of(index * SUB, SUB), count)

    def loads(b):
        lanes = lanes_at(b * TILES, TILES)
        pairs = ((x_hbm, xv), (d_hbm, dv), (g_hbm, gv))
        return [
            pltpu.make_async_copy(src.at[:, lanes], dst.at[:, lanes], load.at[i, b])
            for i, (src, dst) in enumerate(pairs)
        ]

    smalls = [
        pltpu.make_async_copy(src, dst, small_load.at[i])
        for i, (src, dst) in enumerate(((b_hbm, bv), (c_hbm, cv), (a_hbm, av)))
    ]
    for small in smalls:
        small.start()
    for b in range(blocks):
        for each in loads(b):
            each.start()

    def tell(i):
        for k in range(SUB):
            pl.semaphore_signal(
                barrier, inc=1, device_id=(lax.rem(me + 1 + i * SUB + k, n),),
                device_id_type=MESH,
            )

    loop(0, n // SUB, tell)
    for small in smalls[:2]:
        small.wait()
    for t in range(tokens):
        bx[t] = jnp.broadcast_to(bv[:, t : t + 1], (n_state, LANES))
        cx[t] = jnp.broadcast_to(cv[:, t : t + 1], (n_state, LANES))
    smalls[2].wait()
    for k in range(all_tiles):
        rt[k] = av[:, k * LANES : (k + 1) * LANES] * (-LOG2E)

    def clear(i):
        for s in range(GROUP):
            accb[i * GROUP + s] = jnp.zeros((n_state, LANES), F32)
            accc[i * GROUP + s] = jnp.zeros((n_state, LANES), F32)

    loop(0, tokens // GROUP, clear)
    zero = jnp.zeros((TILES, n_state, LANES), F32)

    def other(k):
        far = me + 1 + k
        return jnp.where(far >= n, far - n, far)

    def give1(c, k):
        dest = other(k)
        copy(
            out1.at[c, slot(dest, 3)], in1.at[c, slot(me, 3)], send1.at[c], recv1.at[c], dest
        ).start()

    def give2(c, k):
        dest = other(k)
        copy(
            out2.at[c, slot(dest, 2)], in2.at[c, slot(me, 2)], send2.at[c], recv2.at[c], dest
        ).start()

    def give3(b, k):
        dest = b * TILES * parts + k
        mine = dest == me
        to = jnp.where(mine, partner, dest)
        at = jnp.where(mine, n, me)
        copy(out3.at[dest], in3.at[at], send3.at[0], recv3.at[0], to).start()

    def burst(emit):
        def body(i):
            for s in range(14):
                emit(i * 14 + s)

        loop(0, (n - 2) // 14, body)
        emit(n - 2)

    def summarize(b):
        first = b * TILES
        for each in loads(b):
            each.wait()
        for k in range(TILES):
            lanes = lanes_at(first + k)
            delta = dv[:, lanes].astype(F32)
            dl[first + k] = delta
            uu[first + k] = delta * xv[:, lanes].astype(F32)
            gg[first + k] = gv[:, lanes].astype(F32)

        def forth(i, end):
            rates = rt[pl.ds(first, TILES)]
            for s in range(FORTH):
                t = i * FORTH + s
                decay = jnp.exp2(row(dl, first, t) * rates)
                dec[b, t] = decay
                end = decay * end + bx[t][None] * row(uu, first, t)
            return end

        end = lax.fori_loop(0, tokens // FORTH, forth, zero)
        c = b // chunk_blocks
        base = (b - c * chunk_blocks) * TILES * n_state

        def message(k, r):
            return pl.ds((base + k * n_state) * SUB + r, n_state, stride=SUB)

        for k in range(TILES):
            out1[c, message(k, 0), :] = end[k]
            spent = jnp.sum(dl[first + k], axis=0, keepdims=True)
            out1[c, message(k, 2), :] = jnp.broadcast_to(spent, (n_state, LANES))

        def back(i, later):
            for s in range(BACK):
                t = tokens - 1 - i * BACK - s
                later = dec[b, t] * (cx[t][None] * row(gg, first, t) + later)
            return later

        later = lax.fori_loop(0, tokens // BACK, back, zero)
        for k in range(TILES):
            out1[c, message(k, 1), :] = later[k]

    upper = lax.broadcasted_iota(jnp.int32, (2, LANES), 0) < 1

    def propagate(c):
        settle(in1.at[c, pl.ds(0, 3 * (n - 1))], recv1.at[c])
        in1[c, slot(me, 3), :] = out1[c, slot(me, 3), :]
        own = rt[c * chunk_tiles + me // n_state, pl.ds(lax.rem(me, n_state), 2, stride=0), :]

        def scan(i, state):
            e = n - 1 - i
            out2[c, pl.ds(i * SUB, 1), :] = state[:1]
            out2[c, pl.ds(e * SUB + 1, 1), :] = state[1:]
            spent = jnp.where(
                upper,
                in1[c, pl.ds(i * SUB + 2, 2, stride=0), :],
                in1[c, pl.ds(e * SUB + 2, 2, stride=0), :],
            )
            term = jnp.where(upper, in1[c, slot(i, 2), :], in1[c, slot(e, 2), :])
            return jnp.exp2(own * spent) * state + term

        lax.fori_loop(0, n, scan, jnp.zeros((2, LANES), F32), unroll=8)

    def returned(c):
        settle(in2.at[c, pl.ds(0, 2 * (n - 1))], recv2.at[c])
        in2[c, slot(me, 2), :] = out2[c, slot(me, 2), :]

    lane_group = lax.broadcasted_iota(jnp.int32, (SUB, LANES), 1) // width
    low_lanes = lax.broadcasted_iota(jnp.int32, (SUB // 2, LANES), 1) < LANES // 2

    def differentiate(b):
        first = b * TILES
        c = b // chunk_blocks
        base = (b - c * chunk_blocks) * TILES * n_state

        def incoming(r):
            return jnp.stack([
                in2[c, pl.ds((base + k * n_state) * SUB + r, n_state, stride=SUB), :]
                for k in range(TILES)
            ])

        def ahead(i, hidden):
            for s in range(AHEAD):
                t = i * AHEAD + s
                hs[t] = hidden
                hidden = dec[b, t] * hidden + bx[t][None] * row(uu, first, t)
                accc[t] += jnp.sum(row(gg, first, t) * hidden, axis=0)
            return hidden

        lax.fori_loop(0, tokens // AHEAD, ahead, incoming(0))

        def behind(i, carry):
            later, rate = carry
            rates = rt[pl.ds(first, TILES)]
            start = tokens - PAIR - i * PAIR
            for s in reversed(range(PAIR)):
                t = start + s
                state = cx[t][None] * row(gg, first, t) + later
                later = dec[b, t] * state
                weighted = later * hs[t]
                rate = rate + weighted * row(dl, first, t)
                one, two = state * bx[t][None], weighted * rates
                fold = pl.ds((s // SUB) * SUB * SUB + s % SUB, SUB, stride=SUB)
                for k in range(TILES):
                    csp[k, fold, :] = one[k, :SUB] + one[k, SUB:]
                    awp[k, fold, :] = two[k, :SUB] + two[k, SUB:]
                accb[t] += jnp.sum(state * row(uu, first, t), axis=0)
            tok = pl.ds(pl.multiple_of(start, PAIR), PAIR)

            def folded(ref, k):
                halves = []
                for h in range(PAIR // SUB):
                    pieces = [
                        ref[k, (h * SUB + s) * SUB : (h * SUB + s + 1) * SUB, :]
                        for s in range(SUB)
                    ]
                    while len(pieces) > 1:
                        pieces = [p + q for p, q in zip(pieces[::2], pieces[1::2])]
                    halves.append(pieces[0])
                return jnp.concatenate(halves, axis=0)

            for k in range(TILES):
                coeff, weigh = folded(csp, k), folded(awp, k)
                lanes = lanes_at(first + k)
                x = xv[tok, lanes].astype(F32)
                giv[tok, lanes] = (dl[first + k, tok, :] * coeff).astype(giv.dtype)
                gsv[tok, lanes] = (x * coeff + LN2 * weigh).astype(gsv.dtype)
            return later, rate

        _, rate = lax.fori_loop(0, tokens // PAIR, behind, (incoming(1), zero))
        for k in range(TILES):
            halves = (-rate[k, :SUB], -rate[k, SUB:])
            turned = [
                [v if s == 0 else pltpu.roll(v, s * width, axis=1) for s in range(parts)]
                for v in halves
            ]
            for j in range(parts):
                packed = turned[0][(0 - j) % parts]
                for g in range(1, parts):
                    packed = jnp.where(lane_group == g, turned[g % 2][(g - j) % parts], packed)
                pk[k * parts + j] = packed
        for k in range(TILES):
            for j in range(parts):
                at = k * parts + j
                out3[first * parts + at] = jnp.where(
                    low_lanes, pk[at, : SUB // 2], pk[at, SUB // 2 :]
                )

    for b in range(3):
        summarize(b)
    pl.semaphore_wait(barrier, n)
    burst(partial(give1, 0))
    summarize(3)
    burst(partial(give1, 1))
    for b in range(4, 6):
        summarize(b)
    burst(partial(give1, 2))
    summarize(6)
    propagate(0)
    burst(partial(give2, 0))
    summarize(7)
    burst(partial(give1, 3))
    propagate(1)
    burst(partial(give2, 1))
    propagate(2)
    burst(partial(give2, 2))
    for b in range(blocks):
        if b % chunk_blocks == 0:
            returned(b // chunk_blocks)
        differentiate(b)
        for k in range(TILES * parts):
            give3(b, k)
        if b == 0:
            propagate(3)
            burst(partial(give2, 3))
    in3[me] = out3[me]
    lane_sums(accb, gb_ref, tokens, n_state)
    lane_sums(accc, gc_ref, tokens, n_state)
    settle(in3.at[pl.ds(0, n)], recv3.at[0])
    blank = jnp.zeros((SUB // 2, LANES), F32)
    total = lax.fori_loop(0, n, lambda d, total: total + in3[d], blank, unroll=8)
    gr_ref[0:4, :] = total[:, :width]
    gr_ref[4:8, :] = total[:, 2 * width : 3 * width]
    gr_ref[8:12, :] = total[:, width : 2 * width]
    gr_ref[12:16, :] = total[:, 3 * width :]
    for c in range(CHUNKS):
        settle(out1.at[c, pl.ds(0, 3 * (n - 1))], send1.at[c])
        settle(out2.at[c, pl.ds(0, 2 * (n - 1))], send2.at[c])
    settle(out3.at[pl.ds(0, n)], send3.at[0])


def shards(n, inputs, step_sizes, cotangent, input_coeffs, output_coeffs, decay_rates):
    n_state, channels = decay_rates.shape
    tokens = inputs.shape[0]
    all_tiles = channels // LANES
    blocks = all_tiles // TILES
    parts = n // all_tiles
    wide = pltpu.VMEM((tokens, n_state, LANES), F32)
    flat = pltpu.VMEM((all_tiles, tokens, LANES), F32)
    fold = pltpu.VMEM((TILES, PAIR * SUB, LANES), F32)
    rows = pltpu.VMEM((tokens, channels), jnp.bfloat16)
    coefs = pltpu.VMEM((n_state, tokens), F32)
    vmem = pl.BlockSpec(memory_space=pltpu.VMEM)
    hbm = pl.BlockSpec(memory_space=pl.ANY)
    slots = pltpu.VMEM((CHUNKS, n * SUB, LANES), F32)
    small = pltpu.VMEM((n + 1, SUB // 2, LANES), F32)
    each = pltpu.SemaphoreType.DMA((CHUNKS,))
    one = pltpu.SemaphoreType.DMA((1,))
    outs = [
        jax.ShapeDtypeStruct((tokens, channels), jnp.bfloat16),
        jax.ShapeDtypeStruct((tokens, channels), jnp.bfloat16),
        jax.ShapeDtypeStruct((n_state, tokens), F32),
        jax.ShapeDtypeStruct((n_state, tokens), F32),
        jax.ShapeDtypeStruct((n_state, channels // n), F32),
    ]
    return pl.pallas_call(
        partial(whole_kernel, n),
        name="whole",
        in_specs=[hbm] * 6,
        out_specs=[vmem] * 5,
        out_shape=[pltpu.VMEM(shape.shape, shape.dtype) for shape in outs],
        scratch_shapes=[
            rows, rows, rows, coefs, coefs, pltpu.VMEM((n_state, channels), F32),
            wide, wide, flat, flat, flat,
            pltpu.VMEM((blocks, tokens, TILES, n_state, LANES), F32),
            pltpu.VMEM((tokens, TILES, n_state, LANES), F32),
            wide, wide, fold, fold,
            pltpu.VMEM((all_tiles, n_state, LANES), F32),
            pltpu.VMEM((TILES * parts, SUB, LANES), F32),
            slots, slots, slots, slots, small, small,
            each, each, each, each, one, one,
            pltpu.SemaphoreType.DMA((3, blocks)),
            pltpu.SemaphoreType.DMA((3,)),
        ],
        compiler_params=pltpu.CompilerParams(
            collective_id=0, has_side_effects=True, vmem_limit_bytes=60 * 1024 * 1024
        ),
    )(inputs, step_sizes, cotangent, input_coeffs, output_coeffs, decay_rates)


def solution(mesh):
    placed = (P("seq", None), P("seq", None), P("seq", None), P(None, "seq"), P(None, "seq"), P())
    return jax.shard_map(
        partial(shards, mesh.shape["seq"]),
        mesh=mesh,
        in_specs=placed,
        out_specs=(P("seq", None), P("seq", None), P(None, "seq"), P(None, "seq"), P(None, "seq")),
        check_vma=False,
    )
```

time: 76 us -> 64.6 us (0.85)
  Pallas kernels: 69.8 us -> 60.1 us
  local copies, waits for them, and re-layouts: 5.35 us -> 3.74 us
    pallas_call x1, Pallas kernels: 69.8 us -> 60.1 us  [shards(): pl.pallas_call(partial(whole_kernel, n), name='whole', in_specs=[hbm] * 6...]
    unnamed x13 -> x5, local copies, waits for them, and re-layouts: 5.35 us -> 3.74 us
where the time goes in v2:
time: 64.6 us; the launch traced here: 64.4 us
  Pallas kernels  60.1 us (93%)
  local copies, waits for them, and re-layouts  3.74 us (6%)
    pallas_call x1, Pallas kernels, shards(): pl.pallas_call(partial(whole_kernel, n), name='whole', in_specs=[hbm] * 6...  60.1 us
    unnamed x5, local copies, waits for them, and re-layouts  3.74 us

profile of v2, /device:TPU:31, one launch (start us, length us, event | category | flops | bytes accessed | tf_op | source)
XLA Modules:
  0.0 64.4 jit_solution(2053096791417523341)
XLA Ops:
  0.6 60.1 %whole.1 = (bf16[128,4096]{1,0:T(8,128)(2,1)S(1)}, bf16[128,4096]{1,0:T(8,128)(2,1)S(1)}, f32[16,128]{1,0:T(8,128)S(1)}, f32[16,128]{1,0:T(8,128)S(1)}, f32[16,32]{1,0:T(8,128)S(1)}) custom-call(bf16[128,4096]{1,0:T(8,128)(2,1)} %x_hbm.1, bf16[128,4096]{1,0:T(8,128)(2,1)} %d_hbm.1, bf16[128,4096]{1,0:T(8,128)(2,1)} %g_hbm.1, f32[16,128]{1,0:T(8,128)} %b_hbm.1, ...), custom_call_target="tpu_custom_call" | custom-call | tf_op jit(solution)/shard_map/whole/pallas_call | solution.py:370
  60.7 1.0 %copy.16 = bf16[128,4096]{1,0:T(8,128)(2,1)} copy(bf16[128,4096]{1,0:T(8,128)(2,1)S(1)} %get-tuple-element.5) | data formatting | bytes 2097152
  61.7 0.6 copy.18
  62.3 0.6 copy.19
  62.9 0.6 copy.20
  63.5 1.0 %copy.17 = bf16[128,4096]{1,0:T(8,128)(2,1)} copy(bf16[128,4096]{1,0:T(8,128)(2,1)S(1)} %get-tuple-element.6) | data formatting | bytes 2097152

commit v3 on v2

v3 whole, which is shorter than its diff:
```python
from functools import partial
import math

import jax
import jax.numpy as jnp
from jax import lax
from jax.experimental import pallas as pl
from jax.experimental.pallas import tpu as pltpu
from jax.sharding import PartitionSpec as P

LANES = 128
SUB = 8
TILES = 4
GROUP = 8
FORTH = 32
BACK = 32
AHEAD = 32
PAIR = 32
SWEEP = 32
OCTETS = ((0, 1), (1, 1), (2, 2))
DEFER = 4
LOG2E = math.log2(math.e)
LN2 = math.log(2.0)
F32 = jnp.float32
MESH = pl.DeviceIdType.MESH


def loop(start, stop, body):
    def step(k, _):
        body(k)
        return 0

    lax.fori_loop(start, stop, step, 0)


def lane_sums(acc, out_ref, tokens, n_state):
    lane = lax.broadcasted_iota(jnp.int32, (n_state, tokens), 1)
    total = jnp.zeros((n_state, tokens), F32)
    for t in range(tokens):
        total = jnp.where(lane == t, jnp.sum(acc[t], axis=1, keepdims=True), total)
    out_ref[...] = total


def deliver(*refs):
    sems = refs[-1]
    moves = [
        pltpu.make_async_copy(refs[i], refs[5 + i], sems.at[i]) for i in range(5)
    ]
    for move in moves:
        move.start()
    for move in moves:
        move.wait()


def whole_kernel(
    n,
    x_hbm, d_hbm, g_hbm, b_hbm, c_hbm, a_hbm,
    giv, gsv, gb_ref, gc_ref, gr_ref,
    xv, dv, gv, bv, cv, av,
    bx, cx, dl, uu, gg, dec, hs, accb, accc, csp, awp, rt, rs, pk,
    out1, in1, out2, in2, out3, in3,
    send1, recv1, send2, recv2, send3, recv3, load, small_load,
):
    me = lax.axis_index("seq")
    tokens, channels = xv.shape
    n_state = av.shape[0]
    all_tiles = channels // LANES
    blocks = all_tiles // TILES
    octet = n // n_state
    parts = n // all_tiles
    width = LANES // parts
    partner = me + 1 - 2 * lax.rem(me, 2)
    barrier = pltpu.get_barrier_semaphore()

    def copy(src, dst, send_sem, recv_sem, dest):
        return pltpu.make_async_remote_copy(
            src_ref=src, dst_ref=dst, send_sem=send_sem, recv_sem=recv_sem,
            device_id=(dest,), device_id_type=MESH,
        )

    def other(k):
        far = me + 1 + k
        return jnp.where(far >= n, far - n, far)

    def settle(ref, sem):
        pltpu.make_async_copy(ref, ref, sem).wait()

    def row(ref, first, t):
        return ref[pl.ds(first, TILES), pl.ds(t, n_state, stride=0), :]

    def lanes_at(tile, count=1):
        return pl.ds(pl.multiple_of(tile * LANES, LANES), count * LANES)

    def slot(index, count):
        return pl.ds(pl.multiple_of(index * SUB, SUB), count)

    def loads(b):
        lanes = lanes_at(b * TILES, TILES)
        pairs = ((x_hbm, xv), (d_hbm, dv), (g_hbm, gv))
        return [
            pltpu.make_async_copy(src.at[:, lanes], dst.at[:, lanes], load.at[i, b])
            for i, (src, dst) in enumerate(pairs)
        ]

    smalls = [
        pltpu.make_async_copy(src, dst, small_load.at[i])
        for i, (src, dst) in enumerate(((b_hbm, bv), (c_hbm, cv), (a_hbm, av)))
    ]
    for small in smalls:
        small.start()
    for b in range(blocks):
        for each in loads(b):
            each.start()

    def tell(i):
        for k in range(SUB):
            pl.semaphore_signal(
                barrier, inc=1, device_id=(other(i * SUB + k),),
                device_id_type=MESH,
            )

    loop(0, n // SUB, tell)
    for small in smalls[:2]:
        small.wait()
    for t in range(tokens):
        bx[t] = jnp.broadcast_to(bv[:, t : t + 1], (n_state, LANES))
        cx[t] = jnp.broadcast_to(cv[:, t : t + 1], (n_state, LANES))
    smalls[2].wait()
    for k in range(all_tiles):
        rt[k] = av[:, k * LANES : (k + 1) * LANES] * (-LOG2E)

    def clear(i):
        for s in range(GROUP):
            accb[i * GROUP + s] = jnp.zeros((n_state, LANES), F32)
            accc[i * GROUP + s] = jnp.zeros((n_state, LANES), F32)

    loop(0, tokens // GROUP, clear)
    zero = jnp.zeros((TILES, n_state, LANES), F32)

    def place(b):
        per = octet // TILES
        if isinstance(b, int):
            start = [i for i, (low, count) in enumerate(OCTETS) if low <= b // per][-1]
        else:
            start = len(OCTETS) - 1
        return start, b // per - OCTETS[start][0], lax.rem(b, per) * TILES * n_state

    def give1(c, k):
        dest, rows = other(k), 3 * OCTETS[c][1]
        copy(
            out1.at[c, slot(dest, rows)], in1.at[c, slot(me, rows)],
            send1.at[c], recv1.at[c], dest,
        ).start()

    def give2(c, k):
        dest, rows = other(k), 2 * OCTETS[c][1]
        copy(
            out2.at[c, slot(dest, rows)], in2.at[c, slot(me, rows)],
            send2.at[c], recv2.at[c], dest,
        ).start()

    def give3(k):
        mine = k == me
        to = jnp.where(mine, partner, k)
        at = jnp.where(mine, n, me)
        copy(out3.at[k], in3.at[at], send3.at[0], recv3.at[0], to).start()

    def burst(emit):
        def body(i):
            for s in range(14):
                emit(i * 14 + s)

        loop(0, (n - 2) // 14, body)
        emit(n - 2)

    def summarize(b):
        first = b * TILES
        for each in loads(b):
            each.wait()
        for k in range(TILES):
            lanes = lanes_at(first + k)
            delta = dv[:, lanes].astype(F32)
            dl[first + k] = delta
            uu[first + k] = delta * xv[:, lanes].astype(F32)
            gg[first + k] = gv[:, lanes].astype(F32)

        def forth(i, end):
            rates = rt[pl.ds(first, TILES)]
            for s in range(FORTH):
                t = i * FORTH + s
                decay = jnp.exp2(row(dl, first, t) * rates)
                dec[b, t] = decay
                end = decay * end + bx[t][None] * row(uu, first, t)
            return end

        end = lax.fori_loop(0, tokens // FORTH, forth, zero)
        c, o, base = place(b)
        count = OCTETS[c][1]

        def message(k, r):
            return pl.ds((base + k * n_state) * SUB + r, n_state, stride=SUB)

        for k in range(TILES):
            out1[c, message(k, 2 * o), :] = end[k]
            spent = jnp.sum(dl[first + k], axis=0, keepdims=True)
            out1[c, message(k, 2 * count + o), :] = jnp.broadcast_to(spent, (n_state, LANES))

        def back(i, later):
            for s in range(BACK):
                t = tokens - 1 - i * BACK - s
                later = dec[b, t] * (cx[t][None] * row(gg, first, t) + later)
            return later

        later = lax.fori_loop(0, tokens // BACK, back, zero)
        for k in range(TILES):
            out1[c, message(k, 2 * o + 1), :] = later[k]

    def propagate(c):
        start, count = OCTETS[c]
        run = n // SUB
        settle(in1.at[c, pl.ds(0, 3 * count * (n - 1))], recv1.at[c])
        in1[c, slot(me, 3 * count), :] = out1[c, slot(me, 3 * count), :]
        line = lax.broadcasted_iota(jnp.int32, (SUB, LANES), 0)
        none = jnp.zeros((SUB, LANES), F32)

        def lines(j, r):
            return pl.ds(j * SUB + r, SUB, stride=run * SUB)

        def carried(total, last, shift, edge):
            carry = none
            for _ in range(SUB - 1):
                moved = pltpu.roll(total * carry + last, shift, axis=0)
                carry = jnp.where(line == edge, 0.0, moved)
            return carry

        for o in range(count):
            own = rt[
                (start + o) * octet + me // n_state,
                pl.ds(lax.rem(me, n_state), SUB, stride=0), :
            ]
            decays = [
                jnp.exp2(own * in1[c, lines(j, 2 * count + o), :]) for j in range(run)
            ]
            for r, order, shift, edge in (
                (2 * o, range(run), 1, 0), (2 * o + 1, reversed(range(run)), SUB - 1, SUB - 1)
            ):
                state, product = none, jnp.ones((SUB, LANES), F32)
                kept = []
                for j in order:
                    kept.append((j, state, product))
                    state = decays[j] * state + in1[c, lines(j, r), :]
                    product = decays[j] * product
                carry = carried(product, state, shift, edge)
                for j, local, reach in kept:
                    out2[c, lines(j, r), :] = local + reach * carry

    def returned(c):
        rows = 2 * OCTETS[c][1]
        settle(in2.at[c, pl.ds(0, rows * (n - 1))], recv2.at[c])
        in2[c, slot(me, rows), :] = out2[c, slot(me, rows), :]

    lane_group = lax.broadcasted_iota(jnp.int32, (SUB, LANES), 1) // width
    low_lanes = lax.broadcasted_iota(jnp.int32, (SUB // 2, LANES), 1) < LANES // 2

    def incoming(b, r):
        c, o, base = place(b)
        return jnp.stack([
            in2[c, pl.ds((base + k * n_state) * SUB + 2 * o + r, n_state, stride=SUB), :]
            for k in range(TILES)
        ])

    def restore(b):
        first = b * TILES

        def ahead(i, hidden):
            for s in range(AHEAD):
                t = i * AHEAD + s
                hs[t] = hidden
                hidden = dec[b, t] * hidden + bx[t][None] * row(uu, first, t)
                accc[t] += jnp.sum(row(gg, first, t) * hidden, axis=0)
            return hidden

        lax.fori_loop(0, tokens // AHEAD, ahead, incoming(b, 0))

    def fold_token(first, s, t, state, weighted, rates):
        one, two = state * bx[t][None], weighted * rates
        fold = pl.ds((s // SUB) * SUB * SUB + s % SUB, SUB, stride=SUB)
        for k in range(TILES):
            csp[k, fold, :] = one[k, :SUB] + one[k, SUB:]
            awp[k, fold, :] = two[k, :SUB] + two[k, SUB:]
        accb[t] += jnp.sum(state * row(uu, first, t), axis=0)

    def folded(ref, k):
        halves = []
        for h in range(PAIR // SUB):
            pieces = [
                ref[k, (h * SUB + s) * SUB : (h * SUB + s + 1) * SUB, :] for s in range(SUB)
            ]
            while len(pieces) > 1:
                pieces = [p + q for p, q in zip(pieces[::2], pieces[1::2])]
            halves.append(pieces[0])
        return jnp.concatenate(halves, axis=0)

    def finish(first, start):
        tok = pl.ds(pl.multiple_of(start, PAIR), PAIR)
        for k in range(TILES):
            coeff, weigh = folded(csp, k), folded(awp, k)
            lanes = lanes_at(first + k)
            x = xv[tok, lanes].astype(F32)
            giv[tok, lanes] = (dl[first + k, tok, :] * coeff).astype(giv.dtype)
            gsv[tok, lanes] = (x * coeff + LN2 * weigh).astype(gsv.dtype)

    def differentiate(b):
        first = b * TILES
        restore(b)

        def behind(i, carry):
            later, rate = carry
            rates = rt[pl.ds(first, TILES)]
            start = tokens - PAIR - i * PAIR
            for s in reversed(range(PAIR)):
                t = start + s
                state = cx[t][None] * row(gg, first, t) + later
                later = dec[b, t] * state
                weighted = later * hs[t]
                rate = rate + weighted * row(dl, first, t)
                fold_token(first, s, t, state, weighted, rates)
            finish(first, start)
            return later, rate

        _, rate = lax.fori_loop(0, tokens // PAIR, behind, (incoming(b, 1), zero))
        for k in range(TILES):
            rs[first + k] = -rate[k]

    def sweep(b):
        first = b * TILES
        restore(b)

        def behind(i, carry):
            later, rate = carry
            for s in range(SWEEP):
                t = tokens - 1 - i * SWEEP - s
                state = cx[t][None] * row(gg, first, t) + later
                later = dec[b, t] * state
                weighted = later * hs[t]
                rate = rate + weighted * row(dl, first, t)
                dec[b, t] = state
                dec[b - DEFER, t] = weighted
            return later, rate

        _, rate = lax.fori_loop(0, tokens // SWEEP, behind, (incoming(b, 1), zero))
        for k in range(TILES):
            rs[first + k] = -rate[k]

    def gather(b):
        first = b * TILES

        def body(i):
            rates = rt[pl.ds(first, TILES)]
            start = i * PAIR
            for s in range(PAIR):
                t = start + s
                fold_token(first, s, t, dec[b, t], dec[b - DEFER, t], rates)
            finish(first, start)

        loop(0, tokens // PAIR, body)

    def give_rates(start, stop):
        for tile in range(start * TILES, stop * TILES):
            halves = (rs[tile, :SUB, :], rs[tile, SUB:, :])
            turned = [
                [v if s == 0 else pltpu.roll(v, s * width, axis=1) for s in range(parts)]
                for v in halves
            ]
            for j in range(parts):
                packed = turned[0][(0 - j) % parts]
                for g in range(1, parts):
                    packed = jnp.where(lane_group == g, turned[g % 2][(g - j) % parts], packed)
                pk[(tile - start * TILES) * parts + j] = packed
        for at in range((stop - start) * TILES * parts):
            out3[start * TILES * parts + at] = jnp.where(
                low_lanes, pk[at, : SUB // 2], pk[at, SUB // 2 :]
            )

        def body(i):
            for s in range(16):
                give3(start * TILES * parts + i * 16 + s)

        loop(0, (stop - start) * TILES * parts // 16, body)

    for b in range(3):
        summarize(b)
    pl.semaphore_wait(barrier, n)
    burst(partial(give1, 0))
    summarize(3)
    burst(partial(give1, 1))
    for b in range(4, 6):
        summarize(b)
    summarize(6)
    propagate(0)
    burst(partial(give2, 0))
    summarize(7)
    burst(partial(give1, 2))
    propagate(1)
    burst(partial(give2, 1))
    returned(0)
    differentiate(0)
    differentiate(1)
    propagate(2)
    burst(partial(give2, 2))
    returned(1)
    differentiate(2)
    differentiate(3)
    give_rates(0, DEFER)
    returned(2)
    loop(DEFER, blocks, sweep)
    give_rates(DEFER, blocks)
    loop(DEFER, blocks, gather)
    in3[me] = out3[me]
    lane_sums(accb, gb_ref, tokens, n_state)
    lane_sums(accc, gc_ref, tokens, n_state)
    settle(in3.at[pl.ds(0, n)], recv3.at[0])
    blank = jnp.zeros((SUB // 2, LANES), F32)
    total = lax.fori_loop(0, n, lambda d, total: total + in3[d], blank, unroll=8)
    gr_ref[0:4, :] = total[:, :width]
    gr_ref[4:8, :] = total[:, 2 * width : 3 * width]
    gr_ref[8:12, :] = total[:, width : 2 * width]
    gr_ref[12:16, :] = total[:, 3 * width :]
    for c, (_, count) in enumerate(OCTETS):
        settle(out1.at[c, pl.ds(0, 3 * count * (n - 1))], send1.at[c])
        settle(out2.at[c, pl.ds(0, 2 * count * (n - 1))], send2.at[c])
    settle(out3.at[pl.ds(0, n)], send3.at[0])


def shards(n, inputs, step_sizes, cotangent, input_coeffs, output_coeffs, decay_rates):
    n_state, channels = decay_rates.shape
    tokens = inputs.shape[0]
    all_tiles = channels // LANES
    blocks = all_tiles // TILES
    parts = n // all_tiles
    wide = pltpu.VMEM((tokens, n_state, LANES), F32)
    flat = pltpu.VMEM((all_tiles, tokens, LANES), F32)
    fold = pltpu.VMEM((TILES, PAIR * SUB, LANES), F32)
    rows = pltpu.VMEM((tokens, channels), jnp.bfloat16)
    coefs = pltpu.VMEM((n_state, tokens), F32)
    vmem = pl.BlockSpec(memory_space=pltpu.VMEM)
    hbm = pl.BlockSpec(memory_space=pl.ANY)
    slots = pltpu.VMEM((len(OCTETS), n * SUB, LANES), F32)
    small = pltpu.VMEM((n + 1, SUB // 2, LANES), F32)
    each = pltpu.SemaphoreType.DMA((len(OCTETS),))
    one = pltpu.SemaphoreType.DMA((1,))
    outs = [
        jax.ShapeDtypeStruct((tokens, channels), jnp.bfloat16),
        jax.ShapeDtypeStruct((tokens, channels), jnp.bfloat16),
        jax.ShapeDtypeStruct((n_state, tokens), F32),
        jax.ShapeDtypeStruct((n_state, tokens), F32),
        jax.ShapeDtypeStruct((n_state, channels // n), F32),
    ]
    results = pl.pallas_call(
        partial(whole_kernel, n),
        name="whole",
        in_specs=[hbm] * 6,
        out_specs=[vmem] * 5,
        out_shape=[pltpu.VMEM(shape.shape, shape.dtype) for shape in outs],
        scratch_shapes=[
            rows, rows, rows, coefs, coefs, pltpu.VMEM((n_state, channels), F32),
            wide, wide, flat, flat, flat,
            pltpu.VMEM((blocks, tokens, TILES, n_state, LANES), F32),
            pltpu.VMEM((tokens, TILES, n_state, LANES), F32),
            wide, wide, fold, fold,
            pltpu.VMEM((all_tiles, n_state, LANES), F32),
            pltpu.VMEM((all_tiles, n_state, LANES), F32),
            pltpu.VMEM((DEFER * TILES * parts, SUB, LANES), F32),
            slots, slots, slots, slots, small, small,
            each, each, each, each, one, one,
            pltpu.SemaphoreType.DMA((3, blocks)),
            pltpu.SemaphoreType.DMA((3,)),
        ],
        compiler_params=pltpu.CompilerParams(
            collective_id=0, has_side_effects=True, vmem_limit_bytes=60 * 1024 * 1024
        ),
    )(inputs, step_sizes, cotangent, input_coeffs, output_coeffs, decay_rates)
    return pl.pallas_call(
        deliver,
        name="deliver",
        in_specs=[vmem] * 5,
        out_specs=[hbm] * 5,
        out_shape=outs,
        scratch_shapes=[pltpu.SemaphoreType.DMA((5,))],
        compiler_params=pltpu.CompilerParams(has_side_effects=False, vmem_limit_bytes=1024 * 1024),
    )(*[pltpu.with_memory_space_constraint(r, pltpu.VMEM) for r in results])


def solution(mesh):
    placed = (P("seq", None), P("seq", None), P("seq", None), P(None, "seq"), P(None, "seq"), P())
    return jax.shard_map(
        partial(shards, mesh.shape["seq"]),
        mesh=mesh,
        in_specs=placed,
        out_specs=(P("seq", None), P("seq", None), P(None, "seq"), P(None, "seq"), P(None, "seq")),
        check_vma=False,
    )
```

time: 64.6 us -> 59.2 us (0.916)
  the two profiles are of different devices: /device:TPU:31 before, /device:TPU:1 now
where the time goes in v3:
time: 59.2 us; the launch traced here: 59.1 us
  Pallas kernels  58.4 us (99%)
  between operations  0.64 us (1%)
    pallas_call x1, Pallas kernels, shards(): pl.pallas_call(partial(whole_kernel, n), name='whole', in_specs=[hbm] * 6...  57 us
    pallas_call x1, Pallas kernels, shards(): pl.pallas_call(deliver, name='deliver', in_specs=[vmem] * 5, out_specs=[h...  1.37 us

profile of v3, /device:TPU:1, one launch (start us, length us, event | category | flops | bytes accessed | tf_op | source)
XLA Modules:
  0.0 59.1 jit_solution(4687034878218833350)
XLA Ops:
  0.6 57.0 %whole.1 = (bf16[128,4096]{1,0:T(8,128)(2,1)S(1)}, bf16[128,4096]{1,0:T(8,128)(2,1)S(1)}, f32[16,128]{1,0:T(8,128)S(1)}, f32[16,128]{1,0:T(8,128)S(1)}, f32[16,32]{1,0:T(8,128)S(1)}) custom-call(bf16[128,4096]{1,0:T(8,128)(2,1)} %x_hbm.1, bf16[128,4096]{1,0:T(8,128)(2,1)} %d_hbm.1, bf16[128,4096]{1,0:T(8,128)(2,1)} %g_hbm.1, f32[16,128]{1,0:T(8,128)} %b_hbm.1, ...), custom_call_target="tpu_custom_call" | custom-call | tf_op jit(solution)/shard_map/whole/pallas_call | solution.py:459
  57.7 1.4 %deliver.1 = (bf16[128,4096]{1,0:T(8,128)(2,1)}, bf16[128,4096]{1,0:T(8,128)(2,1)}, f32[16,128]{1,0:T(8,128)}, f32[16,128]{1,0:T(8,128)}, f32[16,32]{1,0:T(8,128)}) custom-call(bf16[128,4096]{1,0:T(8,128)(2,1)S(1)} %get-tuple-element.10.refs_0_, bf16[128,4096]{1,0:T(8,128)(2,1)S(1)} %get-tuple-element.11.refs_1_, f32[16,128]{1,0:T(8,128)S(1)} %get-tuple-element.12.refs_2_, ...), custom_call_target="tpu_custom_call" | custom-call | tf_op jit(solution)/shard_map/deliver/pallas_call | solution.py:483

commit v4 on v3

--- a/solution.py
+++ b/solution.py
@@ -1,4 +1,5 @@
 from functools import partial
+import itertools
 import math
 
 import jax
@@ -22,7 +23,14 @@
 LOG2E = math.log2(math.e)
 LN2 = math.log(2.0)
 F32 = jnp.float32
+SIDES = (4, 4, 4, 2)
 MESH = pl.DeviceIdType.MESH
+
+
+def far_first():
+    steps = list(itertools.product(*(range(side) for side in SIDES)))
+    hops = lambda step: sum(min(s, side - s) for s, side in zip(step[:3], SIDES))
+    return sorted(steps[1:], key=hops, reverse=True)
 
 
 def loop(start, stop, body):
@@ -78,9 +86,17 @@
             device_id=(dest,), device_id_type=MESH,
         )
 
-    def other(k):
-        far = me + 1 + k
-        return jnp.where(far >= n, far - n, far)
+    moved, stride = [], n
+    for side in SIDES:
+        stride //= side
+        here = lax.rem(me // stride, side)
+        moved.append([lax.rem(here + k, side) * stride for k in range(side)])
+    planes = [[p + q for q in moved[1]] for p in moved[0]]
+    cores = [[p + q for q in moved[3]] for p in moved[2]]
+
+    def everyone(emit):
+        for y, x, z, core in far_first():
+            emit(planes[y][x] + cores[z][core])
 
     def settle(ref, sem):
         pltpu.make_async_copy(ref, ref, sem).wait()
@@ -112,14 +128,10 @@
         for each in loads(b):
             each.start()
 
-    def tell(i):
-        for k in range(SUB):
-            pl.semaphore_signal(
-                barrier, inc=1, device_id=(other(i * SUB + k),),
-                device_id_type=MESH,
-            )
-
-    loop(0, n // SUB, tell)
+    def tell(dest):
+        pl.semaphore_signal(barrier, inc=1, device_id=(dest,), device_id_type=MESH)
+
+    everyone(tell)
     for small in smalls[:2]:
         small.wait()
     for t in range(tokens):
@@ -129,12 +141,6 @@
     for k in range(all_tiles):
         rt[k] = av[:, k * LANES : (k + 1) * LANES] * (-LOG2E)
 
-    def clear(i):
-        for s in range(GROUP):
-            accb[i * GROUP + s] = jnp.zeros((n_state, LANES), F32)
-            accc[i * GROUP + s] = jnp.zeros((n_state, LANES), F32)
-
-    loop(0, tokens // GROUP, clear)
     zero = jnp.zeros((TILES, n_state, LANES), F32)
 
     def place(b):
@@ -145,15 +151,15 @@
             start = len(OCTETS) - 1
         return start, b // per - OCTETS[start][0], lax.rem(b, per) * TILES * n_state
 
-    def give1(c, k):
-        dest, rows = other(k), 3 * OCTETS[c][1]
+    def give1(c, dest):
+        rows = 3 * OCTETS[c][1]
         copy(
             out1.at[c, slot(dest, rows)], in1.at[c, slot(me, rows)],
             send1.at[c], recv1.at[c], dest,
         ).start()
 
-    def give2(c, k):
-        dest, rows = other(k), 2 * OCTETS[c][1]
+    def give2(c, dest):
+        rows = 2 * OCTETS[c][1]
         copy(
             out2.at[c, slot(dest, rows)], in2.at[c, slot(me, rows)],
             send2.at[c], recv2.at[c], dest,
@@ -164,14 +170,6 @@
         to = jnp.where(mine, partner, k)
         at = jnp.where(mine, n, me)
         copy(out3.at[k], in3.at[at], send3.at[0], recv3.at[0], to).start()
-
-    def burst(emit):
-        def body(i):
-            for s in range(14):
-                emit(i * 14 + s)
-
-        loop(0, (n - 2) // 14, body)
-        emit(n - 2)
 
     def summarize(b):
         first = b * TILES
@@ -269,26 +267,30 @@
             for k in range(TILES)
         ])
 
+    def gain(acc, t, part, fresh):
+        acc[t] = part if fresh else acc[t] + part
+
     def restore(b):
         first = b * TILES
+        fresh = isinstance(b, int) and b == 0
 
         def ahead(i, hidden):
             for s in range(AHEAD):
                 t = i * AHEAD + s
                 hs[t] = hidden
                 hidden = dec[b, t] * hidden + bx[t][None] * row(uu, first, t)
-                accc[t] += jnp.sum(row(gg, first, t) * hidden, axis=0)
+                gain(accc, t, jnp.sum(row(gg, first, t) * hidden, axis=0), fresh)
             return hidden
 
         lax.fori_loop(0, tokens // AHEAD, ahead, incoming(b, 0))
 
-    def fold_token(first, s, t, state, weighted, rates):
+    def fold_token(first, s, t, state, weighted, rates, fresh=False):
         one, two = state * bx[t][None], weighted * rates
         fold = pl.ds((s // SUB) * SUB * SUB + s % SUB, SUB, stride=SUB)
         for k in range(TILES):
             csp[k, fold, :] = one[k, :SUB] + one[k, SUB:]
             awp[k, fold, :] = two[k, :SUB] + two[k, SUB:]
-        accb[t] += jnp.sum(state * row(uu, first, t), axis=0)
+        gain(accb, t, jnp.sum(state * row(uu, first, t), axis=0), fresh)
 
     def folded(ref, k):
         halves = []
@@ -324,7 +326,7 @@
                 later = dec[b, t] * state
                 weighted = later * hs[t]
                 rate = rate + weighted * row(dl, first, t)
-                fold_token(first, s, t, state, weighted, rates)
+                fold_token(first, s, t, state, weighted, rates, first == 0)
             finish(first, start)
             return later, rate
 
@@ -382,32 +384,27 @@
                 low_lanes, pk[at, : SUB // 2], pk[at, SUB // 2 :]
             )
 
-        def body(i):
-            for s in range(16):
-                give3(start * TILES * parts + i * 16 + s)
-
-        loop(0, (stop - start) * TILES * parts // 16, body)
-
-    for b in range(3):
+        for at in range((stop - start) * TILES * parts):
+            give3(start * TILES * parts + at)
+
+    for b in range(4):
         summarize(b)
-    pl.semaphore_wait(barrier, n)
-    burst(partial(give1, 0))
-    summarize(3)
-    burst(partial(give1, 1))
-    for b in range(4, 6):
+    pl.semaphore_wait(barrier, n - 1)
+    everyone(partial(give1, 0))
+    everyone(partial(give1, 1))
+    for b in range(4, 7):
         summarize(b)
-    summarize(6)
     propagate(0)
-    burst(partial(give2, 0))
+    everyone(partial(give2, 0))
     summarize(7)
-    burst(partial(give1, 2))
+    everyone(partial(give1, 2))
     propagate(1)
-    burst(partial(give2, 1))
+    everyone(partial(give2, 1))
     returned(0)
     differentiate(0)
     differentiate(1)
     propagate(2)
-    burst(partial(give2, 2))
+    everyone(partial(give2, 2))
     returned(1)
     differentiate(2)
     differentiate(3)

time: 59.2 us -> 58.7 us (level)
  no operation moved by 1% of the time
where the time goes in v4:
time: 58.7 us; the launch traced here: 58.6 us
  Pallas kernels  57.9 us (99%)
  between operations  0.64 us (1%)
    pallas_call x1, Pallas kernels, shards(): pl.pallas_call(partial(whole_kernel, n), name='whole', in_specs=[hbm] * 6...  56.6 us
    pallas_call x1, Pallas kernels, shards(): pl.pallas_call(deliver, name='deliver', in_specs=[vmem] * 5, out_specs=[h...  1.37 us

profile of v4, /device:TPU:1, one launch (start us, length us, event | category | flops | bytes accessed | tf_op | source)
XLA Modules:
  0.0 58.6 jit_solution(15203649395438760516)
XLA Ops:
  0.6 56.6 %whole.1 = (bf16[128,4096]{1,0:T(8,128)(2,1)S(1)}, bf16[128,4096]{1,0:T(8,128)(2,1)S(1)}, f32[16,128]{1,0:T(8,128)S(1)}, f32[16,128]{1,0:T(8,128)S(1)}, f32[16,32]{1,0:T(8,128)S(1)}) custom-call(bf16[128,4096]{1,0:T(8,128)(2,1)} %x_hbm.1, bf16[128,4096]{1,0:T(8,128)(2,1)} %d_hbm.1, bf16[128,4096]{1,0:T(8,128)(2,1)} %g_hbm.1, f32[16,128]{1,0:T(8,128)} %b_hbm.1, ...), custom_call_target="tpu_custom_call" | custom-call | tf_op jit(solution)/shard_map/whole/pallas_call | solution.py:456
  57.2 1.4 %deliver.1 = (bf16[128,4096]{1,0:T(8,128)(2,1)}, bf16[128,4096]{1,0:T(8,128)(2,1)}, f32[16,128]{1,0:T(8,128)}, f32[16,128]{1,0:T(8,128)}, f32[16,32]{1,0:T(8,128)}) custom-call(bf16[128,4096]{1,0:T(8,128)(2,1)S(1)} %get-tuple-element.10.refs_0_, bf16[128,4096]{1,0:T(8,128)(2,1)S(1)} %get-tuple-element.11.refs_1_, f32[16,128]{1,0:T(8,128)S(1)} %get-tuple-element.12.refs_2_, ...), custom_call_target="tpu_custom_call" | custom-call | tf_op jit(solution)/shard_map/deliver/pallas_call | solution.py:480

commit v5 on v4

--- a/solution.py
+++ b/solution.py
@@ -24,6 +24,7 @@
 LN2 = math.log(2.0)
 F32 = jnp.float32
 SIDES = (4, 4, 4, 2)
+PIECES = 4
 MESH = pl.DeviceIdType.MESH
 
 
@@ -51,9 +52,15 @@
 
 def deliver(*refs):
     sems = refs[-1]
-    moves = [
-        pltpu.make_async_copy(refs[i], refs[5 + i], sems.at[i]) for i in range(5)
-    ]
+    moves = []
+    for i in range(5):
+        pieces = PIECES if i < 2 else 1
+        rows = refs[i].shape[0] // pieces
+        for p in range(pieces):
+            part = pl.ds(p * rows, rows)
+            moves.append(
+                pltpu.make_async_copy(refs[i].at[part], refs[5 + i].at[part], sems.at[i, p])
+            )
     for move in moves:
         move.start()
     for move in moves:
@@ -387,16 +394,18 @@
         for at in range((stop - start) * TILES * parts):
             give3(start * TILES * parts + at)
 
-    for b in range(4):
+    for b in range(3):
         summarize(b)
     pl.semaphore_wait(barrier, n - 1)
     everyone(partial(give1, 0))
+    summarize(3)
     everyone(partial(give1, 1))
-    for b in range(4, 7):
+    for b in range(4, 6):
         summarize(b)
     propagate(0)
     everyone(partial(give2, 0))
-    summarize(7)
+    for b in range(6, 8):
+        summarize(b)
     everyone(partial(give1, 2))
     propagate(1)
     everyone(partial(give2, 1))
@@ -483,7 +492,7 @@
         in_specs=[vmem] * 5,
         out_specs=[hbm] * 5,
         out_shape=outs,
-        scratch_shapes=[pltpu.SemaphoreType.DMA((5,))],
+        scratch_shapes=[pltpu.SemaphoreType.DMA((5, PIECES))],
         compiler_params=pltpu.CompilerParams(has_side_effects=False, vmem_limit_bytes=1024 * 1024),
     )(*[pltpu.with_memory_space_constraint(r, pltpu.VMEM) for r in results])
 

time: 58.7 us -> 57.5 us (0.980)
  Pallas kernels: 57.9 us -> 56.8 us
    pallas_call x1, Pallas kernels: 56.6 us -> 55.3 us  [shards(): pl.pallas_call(partial(whole_kernel, n), name='whole', in_specs=[hbm] * 6...]
where the time goes in v5:
time: 57.5 us; the launch traced here: 57.4 us
  Pallas kernels  56.8 us (99%)
  between operations  0.64 us (1%)
    pallas_call x1, Pallas kernels, shards(): pl.pallas_call(partial(whole_kernel, n), name='whole', in_specs=[hbm] * 6...  55.3 us
    pallas_call x1, Pallas kernels, shards(): pl.pallas_call(deliver, name='deliver', in_specs=[vmem] * 5, out_specs=[h...  1.49 us

profile of v5, /device:TPU:1, one launch (start us, length us, event | category | flops | bytes accessed | tf_op | source)
XLA Modules:
  0.0 57.4 jit_solution(5746966483353281510)
XLA Ops:
  0.6 55.3 %whole.1 = (bf16[128,4096]{1,0:T(8,128)(2,1)S(1)}, bf16[128,4096]{1,0:T(8,128)(2,1)S(1)}, f32[16,128]{1,0:T(8,128)S(1)}, f32[16,128]{1,0:T(8,128)S(1)}, f32[16,32]{1,0:T(8,128)S(1)}) custom-call(bf16[128,4096]{1,0:T(8,128)(2,1)} %x_hbm.1, bf16[128,4096]{1,0:T(8,128)(2,1)} %d_hbm.1, bf16[128,4096]{1,0:T(8,128)(2,1)} %g_hbm.1, f32[16,128]{1,0:T(8,128)} %b_hbm.1, ...), custom_call_target="tpu_custom_call" | custom-call | tf_op jit(solution)/shard_map/whole/pallas_call | solution.py:465
  55.9 1.5 %deliver.1 = (bf16[128,4096]{1,0:T(8,128)(2,1)}, bf16[128,4096]{1,0:T(8,128)(2,1)}, f32[16,128]{1,0:T(8,128)}, f32[16,128]{1,0:T(8,128)}, f32[16,32]{1,0:T(8,128)}) custom-call(bf16[128,4096]{1,0:T(8,128)(2,1)S(1)} %get-tuple-element.10.refs_0_, bf16[128,4096]{1,0:T(8,128)(2,1)S(1)} %get-tuple-element.11.refs_1_, f32[16,128]{1,0:T(8,128)S(1)} %get-tuple-element.12.refs_2_, ...), custom_call_target="tpu_custom_call" | custom-call | tf_op jit(solution)/shard_map/deliver/pallas_call | solution.py:489
